TPU v7x, 128 devices: a whole 4x4x4 slice. The times are simulated.
128 devices in a mesh: dp: 32 (over x, y, core), group: 4 (over z).
Axes of the slice: x: 4, y: 4, z: 4, core: 2. Of those that a mesh axis runs over, the one named last changes fastest.
Arguments:
- images: bfloat16 [16384, 512], P(('dp', 'group')), may hold values from -1 to 1
- texts: bfloat16 [16384, 512], P(('dp', 'group')), may hold values from -1 to 1
- log_scale: float32 [], replicated, may hold values from 2 to 2.7
Outputs:
- grad_images: bfloat16 [16384, 512], P(('dp', 'group'))
- grad_texts: bfloat16 [16384, 512], P(('dp', 'group'))
- loss: float32 [], replicated
- grad_scale: float32 [], replicated
All inputs are finite; a program needn't handle non-finite values.
Results may differ from a plain program's by a relative error of at most 0.0013.
The roundings to bfloat16 on the way count: a program that leaves them out, or rounds other values in their place, can miss the bound.
Values may be sent and summed in bfloat16 or wider, within the bound.
No kernel may reach another device: no remote copies, remote signals or barrier semaphores. Data moves between devices by JAX's collectives and lax.ppermute only.
A program may use at most 128 MiB of HBM per device.

v0:
```python
import jax
import jax.numpy as jnp
from jax import lax
from jax.sharding import Mesh
from jax.sharding import PartitionSpec as P

DP_GROUP = ("dp_0", "dp_1", "dp_2", "group")


def in_one_piece(arrays, axis, split_dim, concat_dim, along):
    ends, at = ([], 0)
    for a in arrays[:-1]:
        at += a.shape[along]
        ends.append(at)
    both = jnp.concatenate(arrays, axis=along)
    return tuple(
        jnp.split(
            lax.all_to_all(both, axis, split_axis=split_dim, concat_axis=concat_dim, tiled=True),
            ends,
            axis=along,
        )
    )


def rows_first(arrays, axis, dims):
    turned = [jnp.moveaxis(a, dim, 0) for a, dim in zip(arrays, dims)]
    both = jnp.concatenate([t.reshape(len(t), -1) for t in turned], axis=1)
    filled, at, outs = (lax.all_gather(both, axis, axis=0, tiled=True), 0, [])
    for t, dim in zip(turned, dims):
        share = filled[:, at : at + t[0].size].reshape(-1, *t.shape[1:])
        outs.append(jnp.moveaxis(share, 0, dim))
        at += t[0].size
    return tuple(outs)


def one_axis_at_a_time(value, axes):
    for axis in axes:
        value = lax.psum(value, axis)
    return value


def body(images, texts, log_scale):
    row_count = images.shape[0]
    device_count = lax.axis_size(DP_GROUP)
    pair_total = row_count * device_count
    texts_whole = lax.all_gather(texts, DP_GROUP, axis=0, tiled=True)
    images_whole = lax.all_gather(images, DP_GROUP, axis=0, tiled=True)
    logit_scale = jnp.exp(log_scale)
    first_pair = lax.axis_index(DP_GROUP) * row_count
    contract_last = (((1,), (1,)), ((), ()))
    contract_first = (((0,), (0,)), ((), ()))
    row_logits = logit_scale * lax.dot_general(
        images, texts_whole, contract_last, preferred_element_type=jnp.float32
    )
    row_top = jnp.max(row_logits, axis=1)
    row_lse = row_top + jnp.log(jnp.sum(jnp.exp(row_logits - row_top[:, None]), axis=1))
    paired = jnp.diagonal(lax.dynamic_slice_in_dim(row_logits, first_pair, row_count, 1))
    part_top = jnp.max(row_logits, axis=0)
    part_sum = jnp.sum(jnp.exp(row_logits - part_top[None, :]), axis=0)
    got_top, got_sum = in_one_piece(
        (part_top.reshape(device_count, row_count), part_sum.reshape(device_count, row_count)),
        DP_GROUP,
        0,
        0,
        1,
    )
    col_top = jnp.max(got_top, axis=0)
    col_lse = col_top + jnp.log(jnp.sum(got_sum * jnp.exp(got_top - col_top[None, :]), axis=0))
    row_whole, col_whole = rows_first((row_lse, col_lse), DP_GROUP, (0, 0))
    own_pairs = (
        jnp.arange(pair_total)[None, :] == (first_pair + jnp.arange(row_count))[:, None]
    ).astype(jnp.float32)
    row_grad = (
        0.5 * (jnp.exp(row_logits - row_lse[:, None]) + jnp.exp(row_logits - col_whole[None, :]))
        - own_pairs
    )
    scale_part = jnp.sum(row_grad * row_logits)
    row_weights = row_grad.astype(jnp.bfloat16)
    grad_images = (
        logit_scale * jnp.dot(row_weights, texts_whole, preferred_element_type=jnp.float32)
    ).astype(jnp.bfloat16)
    col_logits = logit_scale * lax.dot_general(
        images_whole, texts, contract_last, preferred_element_type=jnp.float32
    )
    col_grad = (
        0.5 * (jnp.exp(col_logits - row_whole[:, None]) + jnp.exp(col_logits - col_lse[None, :]))
        - own_pairs.T
    )
    text_sum = logit_scale * lax.dot_general(
        col_grad.astype(jnp.bfloat16),
        images_whole,
        contract_first,
        preferred_element_type=jnp.float32,
    )
    grad_texts = text_sum.astype(jnp.bfloat16)
    loss_part = jnp.sum(row_lse) + jnp.sum(col_lse) - 2.0 * jnp.sum(paired)
    loss_total, scale_total = (
        one_axis_at_a_time(loss_part, DP_GROUP),
        one_axis_at_a_time(scale_part, DP_GROUP),
    )
    return (grad_images, grad_texts, loss_total / (2.0 * pair_total), scale_total / pair_total)


def solution(mesh):
    split = Mesh(
        mesh.devices.reshape(4, 4, 2, mesh.shape["group"]), ("dp_0", "dp_1", "dp_2", "group")
    )
    placed = (P(DP_GROUP, None), P(DP_GROUP, None), P())
    return jax.shard_map(
        body,
        mesh=split,
        in_specs=placed,
        out_specs=(P(DP_GROUP, None), P(DP_GROUP, None), P(), P()),
        check_vma=False,
    )
```

profile of v0, /device:TPU:0, one launch (start us, length us, event | category | flops | bytes accessed | tf_op | source)
XLA Modules:
  0.0 263.8 jit_solution(17786985613269034500)
XLA Ops:
  7.2 0.0 all-gather.3.cloned.1.call-start
  7.2 0.7 all-gather.3.cloned.1.call-update
  7.9 0.0 all-gather.5.cloned.1.call-start
  7.9 0.7 all-gather.5.cloned.1.call-update
  9.4 84.2 %all-gather.3.cloned.1.call-done = bf16[16384,512]{1,0:T(8,128)(2,1)} async-done(((bf16[128,512]{1,0:T(8,128)(2,1)}), bf16[16384,512]{1,0:T(8,128)(2,1)}) %all-gather.3.cloned.1.call-update) | async-done | bytes 16777232 | tf_op jit(solution)/shard_map/all_gather | solution.py:46
  93.6 14.5 %fusion.19 = (f32[128]{0:T(128)S(1)}, f32[16384]{0:T(1024)S(1)}, f32[128,16384]{1,0:T(8,128)}) fusion(bf16[128,512]{1,0:T(8,128)(2,1)} %param.3, bf16[16384,512]{1,0:T(8,128)(2,1)} %all-gather.3.cloned.1.call-done, f32[]{:T(128)S(6)} %exp.24), kind=kOutput, calls=%fused_computation.34 | convolution fusion | flops 2153758720 | bytes 25362948 | tf_op jit(solution)/shard_map/dot_general | solution.py:52
  108.1 4.7 %exponential_reduce_fusion.1 = (f32[128]{0:T(128)S(1)}, f32[16384]{0:T(1024)S(1)}) fusion(f32[128,16384]{1,0:T(8,128)} %get-tuple-element.22, f32[128]{0:T(128)S(1)} %get-tuple-element.6, f32[16384]{0:T(1024)S(1)} %get-tuple-element.7), kind=kLoop, calls=%fused_computation.9 | loop fusion | flops 8372096 | bytes 8520704 | tf_op jit(solution)/shard_map/reduce_sum | solution.py:56
  112.9 0.7 all_to_all.8
  113.6 8.2 %all-to-all-start = ((f32[128,1,256]{2,1,0:T(1,128)}), f32[128,1,256]{2,1,0:T(1,128)S(1)}, u32[]{:S(2)}, u32[]{:S(2)}) async-start(f32[128,1,256]{2,1,0:T(1,128)} %all_to_all.8), calls=%async_computation | async-start | bytes 262144 | tf_op jit(solution)/shard_map/all_to_all | solution.py:18
  121.9 0.9 constant_dynamic-slice_fusion
  122.7 1.2 gather_fusion
  124.0 0.6 reduce_sum.68
  125.2 0.6 fusion.21
  125.8 5.2 %all-to-all-done = f32[128,1,256]{2,1,0:T(1,128)S(1)} async-done(((f32[128,1,256]{2,1,0:T(1,128)}), f32[128,1,256]{2,1,0:T(1,128)S(1)}, u32[]{:S(2)}, u32[]{:S(2)}) %all-to-all-start) | async-done | bytes 131104 | tf_op jit(solution)/shard_map/all_to_all | solution.py:18
  131.1 0.6 fusion.20
  133.1 50.5 %all_gather.10 = f32[16384,2]{0,1:T(2,128)S(1)} all-gather(f32[128,2]{0,1:T(2,128)S(1)} %pad_maximum_fusion.1), channel_id=1, replica_groups=mesh['dp_0'=4,'dp_1'=4,'dp_2'=2,'group'=4] {'dp_0','dp_1','dp_2','group'}, dimensions={0}, use_global_device_ids=true | all-gather | bytes 132096 | tf_op jit(solution)/shard_map/all_gather | solution.py:28
  183.6 0.1 fusion.22
  183.7 6.5 %multiply_reduce_fusion = f32[]{:T(128)} fusion(f32[128,16384]{1,0:T(8,128)} %get-tuple-element.22, s32[128]{0:T(128)S(1)} %iota_add_fusion, f32[16384]{0:T(1024)S(1)} %bitcast.20, f32[128]{0:T(128)S(1)} %get-tuple-element.19), kind=kLoop, calls=%fused_computation.3 | loop fusion | flops 18874368 | bytes 8455172 | tf_op jit(solution)/shard_map/reduce_sum | solution.py:77
  190.2 10.4 %all-reduce.2 = (f32[]{:T(128)}, f32[]{:T(128)}) all-reduce(f32[]{:T(128)S(6)} %sub.87, f32[]{:T(128)} %multiply_reduce_fusion), channel_id=1, replica_groups=mesh['dp_0'=4,'dp_1'=4,'dp_2'=2,'group'=4] {'dp_0'}, use_global_device_ids=true, to_apply=%region_9.10 | all-reduce | flops 2 | bytes 16 | tf_op jit(solution)/shard_map/psum | solution.py:38
  200.6 8.8 %all-reduce.1 = (f32[]{:T(128)}, f32[]{:T(128)}) all-reduce(f32[]{:T(128)} %get-tuple-element.12, f32[]{:T(128)} %get-tuple-element.13), channel_id=1, replica_groups=mesh['dp_0'=4,'dp_1'=4,'dp_2'=2,'group'=4] {'dp_1'}, use_global_device_ids=true, to_apply=%region_10.11 | all-reduce | flops 2 | bytes 16 | tf_op jit(solution)/shard_map/psum | solution.py:38
  209.3 3.1 %all-reduce.3 = (f32[]{:T(128)}, f32[]{:T(128)}) all-reduce(f32[]{:T(128)} %get-tuple-element.10, f32[]{:T(128)} %get-tuple-element.11), channel_id=1, replica_groups=mesh['dp_0'=4,'dp_1'=4,'dp_2'=2,'group'=4] {'dp_2'}, use_global_device_ids=true, to_apply=%region_11.12 | all-reduce | flops 2 | bytes 16 | tf_op jit(solution)/shard_map/psum | solution.py:38
  212.4 10.0 %all-reduce = (f32[]{:T(128)}, f32[]{:T(128)}) all-reduce(f32[]{:T(128)} %get-tuple-element.14, f32[]{:T(128)} %get-tuple-element.15), channel_id=1, replica_groups=mesh['dp_0'=4,'dp_1'=4,'dp_2'=2,'group'=4] {'group'}, use_global_device_ids=true, to_apply=%region_12.13 | all-reduce | flops 2 | bytes 16 | tf_op jit(solution)/shard_map/psum | solution.py:38
  223.8 0.0 copy-start
  223.8 12.4 %fusion.12 = bf16[128,512]{1,0:T(8,128)(2,1)} fusion(bf16[16384,512]{1,0:T(8,128)(2,1)} %all-gather.3.cloned.1.call-done, f32[128,16384]{1,0:T(8,128)} %get-tuple-element.22, s32[128]{0:T(128)S(1)} %iota_add_fusion, f32[16384]{0:T(1024)S(1)} %bitcast.21, f32[128]{0:T(128)S(1)} %get-tuple-element.19, f32[]{:T(128)S(6)} %exp.24), kind=kOutput, calls=%fused_computation.19 | convolution fusion | flops 2164391936 | bytes 25363460 | tf_op jit(solution)/shard_map/dot_general | solution.py:80
  236.2 0.0 all-gather.5.cloned.1.call-done
  236.2 0.0 copy-done
  236.2 18.5 %fusion.15 = bf16[128,512]{1,0:T(8,128)(2,1)} fusion(bf16[16384,512]{1,0:T(8,128)(2,1)} %all-gather.5.cloned.1.call-done, bf16[128,512]{1,0:T(8,128)(2,1)S(1)} %copy-done, s32[128]{0:T(128)S(1)} %iota_add_fusion, f32[128]{0:T(128)S(1)} %get-tuple-element.17, f32[16384]{0:T(1024)S(1)} %bitcast.23, f32[]{:T(128)S(6)} %exp.24), kind=kOutput, calls=%fused_computation.20 | convolution fusion | flops 4313972736 | bytes 17105924 | tf_op jit(solution)/shard_map/dot_general | solution.py:89
  (7 shorter events, 0.1 us)
Async XLA Ops:
  7.2 86.4 %all-gather.3.cloned.1.call-start = ((), (), s32[]{:S(2)}) async-start(), calls=%async_computation.1 | async-start | bytes 16908288 | tf_op jit(solution)/shard_map/all_gather | solution.py:46
  7.9 228.3 %all-gather.5.cloned.1.call-start = ((), (), s32[]{:S(2)}) async-start(), calls=%async_computation.2 | async-start | bytes 16908288 | tf_op jit(solution)/shard_map/all_gather | solution.py:47
  113.6 17.4 %all-to-all-start = ((f32[128,1,256]{2,1,0:T(1,128)}), f32[128,1,256]{2,1,0:T(1,128)S(1)}, u32[]{:S(2)}, u32[]{:S(2)}) async-start(f32[128,1,256]{2,1,0:T(1,128)} %all_to_all.8), calls=%async_computation | async-start | bytes 262144 | tf_op jit(solution)/shard_map/all_to_all | solution.py:18
  223.8 12.4 %copy-start = (bf16[128,512]{1,0:T(8,128)(2,1)S(1)}, bf16[128,512]{1,0:T(8,128)(2,1)}, u32[]{:S(2)}) copy-start(bf16[128,512]{1,0:T(8,128)(2,1)} %param.4) | copy-start | bytes 393220
Sparse Core Ops, SparseCore 0:
  11.1 82.4 all-gather.2
  96.7 79.5 all-gather.4
where the time goes:
time: 264 us
  waiting for transfers between devices  90.8 us (34%)
  blocking collectives  82.8 us (31%)
  matrix products  45.4 us (17%)
  between operations  20.3 us (8%)
  other arithmetic  13.2 us (5%)
  starting transfers between devices  8.3 us (3%)
  local copies, waits for them, and re-layouts  2.96 us (1%)
    all_gather x1, waiting for transfers between devices, body(): texts_whole = lax.all_gather(texts, DP_GROUP, axis=0, tiled=True)  84.2 us
    all_gather x1, blocking collectives, rows_first(): filled, at, outs = (lax.all_gather(both, axis, axis=0, tiled=True), 0, [])  50.5 us
    psum x4, blocking collectives, one_axis_at_a_time(): value = lax.psum(value, axis)  32.3 us
    dot_general x1, matrix products, body(): lax.dot_general(col_grad.astype(jnp.bfloat16), images_whole, contract_fir...  18.5 us
    dot_general x1, matrix products, body(): lax.dot_general(images, texts_whole, contract_last, preferred_element_typ...  14.5 us
    dot_general x1, matrix products, body(): jnp.dot(row_weights, texts_whole, preferred_element_type=jnp.float32)  12.4 us
    all_to_all x1, starting transfers between devices, in_one_piece(): lax.all_to_all(both, axis, split_axis=split_dim, concat_axis=concat_dim,...  8.23 us
    reduce_sum x1, other arithmetic, body(): scale_part = jnp.sum(row_grad * row_logits)  6.49 us
  transfers between devices with their start and end apart: 3, of which 2 were waited for; matrix products, arithmetic and copies ran while one was open for 16% of the time, Pallas kernels for 0%

commit v1 on v0

--- a/solution.py
+++ b/solution.py
@@ -43,7 +43,9 @@
     row_count = images.shape[0]
     device_count = lax.axis_size(DP_GROUP)
     pair_total = row_count * device_count
-    texts_whole = lax.all_gather(texts, DP_GROUP, axis=0, tiled=True)
+    texts_whole = jnp.concatenate(
+        lax.all_to_all(jnp.stack([texts] * lax.axis_size(DP_GROUP)), DP_GROUP, 0, 0), axis=0
+    )
     images_whole = lax.all_gather(images, DP_GROUP, axis=0, tiled=True)
     logit_scale = jnp.exp(log_scale)
     first_pair = lax.axis_index(DP_GROUP) * row_count

time: 264 us -> 445 us (1.69)
  waiting for transfers between devices: 90.8 us -> 248 us
  starting transfers between devices: 8.3 us -> 27.4 us
  local copies, waits for them, and re-layouts: 2.96 us -> 9.67 us
    all_to_all x0 -> x1, waiting for transfers between devices: none -> 242 us  [body(): lax.all_to_all(jnp.stack([texts] * lax.axis_size(DP_GROUP)), DP_GROUP, 0, 0)]
    all_gather x1 -> x0, waiting for transfers between devices: 84.2 us -> none  [body(): texts_whole = lax.all_gather(texts, DP_GROUP, axis=0, tiled=True)]
    all_to_all x0 -> x1, starting transfers between devices: none -> 11.7 us  [body(): lax.all_to_all(jnp.stack([texts] * lax.axis_size(DP_GROUP)), DP_GROUP, 0, 0)]
    all_to_all x1, starting transfers between devices: 8.23 us -> 15.6 us  [in_one_piece(): lax.all_to_all(both, axis, split_axis=split_dim, concat_axis=concat_dim,...]
    another operation x0 -> x1, local copies, waits for them, and re-layouts: none -> 6.7 us  [body(): jnp.stack([texts] * lax.axis_size(DP_GROUP))]
  transfers between devices with their start and end apart: 3 -> 3, of which waited for: 2 -> 2; matrix products, arithmetic and copies ran while one was open for 16% -> 11% of each run, Pallas kernels for 0% -> 0%
where the time goes in v1:
time: 445 us; the launch traced here: 444 us
  waiting for transfers between devices  248 us (56%)
  blocking collectives  80.1 us (18%)
  matrix products  45.5 us (10%)
  starting transfers between devices  27.4 us (6%)
  between operations  20.3 us (5%)
  other arithmetic  13.2 us (3%)
  local copies, waits for them, and re-layouts  9.67 us (2%)
    all_to_all x1, waiting for transfers between devices, body(): lax.all_to_all(jnp.stack([texts] * lax.axis_size(DP_GROUP)), DP_GROUP, 0, 0)  242 us
    all_gather x1, blocking collectives, rows_first(): filled, at, outs = (lax.all_gather(both, axis, axis=0, tiled=True), 0, [])  47.8 us
    psum x4, blocking collectives, one_axis_at_a_time(): value = lax.psum(value, axis)  32.4 us
    dot_general x1, matrix products, body(): lax.dot_general(col_grad.astype(jnp.bfloat16), images_whole, contract_fir...  18.5 us
    all_to_all x1, starting transfers between devices, in_one_piece(): lax.all_to_all(both, axis, split_axis=split_dim, concat_axis=concat_dim,...  15.6 us
    dot_general x1, matrix products, body(): lax.dot_general(images, texts_whole, contract_last, preferred_element_typ...  14.6 us
    dot_general x1, matrix products, body(): jnp.dot(row_weights, texts_whole, preferred_element_type=jnp.float32)  12.4 us
    all_to_all x1, starting transfers between devices, body(): lax.all_to_all(jnp.stack([texts] * lax.axis_size(DP_GROUP)), DP_GROUP, 0, 0)  11.7 us
  transfers between devices with their start and end apart: 3, of which 2 were waited for; matrix products, arithmetic and copies ran while one was open for 11% of the time, Pallas kernels for 0%

profile of v1, /device:TPU:0, one launch (start us, length us, event | category | flops | bytes accessed | tf_op | source)
XLA Modules:
  0.0 444.2 jit_solution(16378072612578555267)
XLA Ops:
  7.2 0.0 all-gather.2.cloned.1.call-start
  7.2 0.7 all-gather.2.cloned.1.call-update
  7.9 6.7 %stack.2 = bf16[128,128,512]{2,1,0:T(8,128)(2,1)} broadcast(bf16[128,512]{1,0:T(8,128)(2,1)} %param.4), dimensions={1,2} | broadcast | bytes 16908288 | tf_op jit(solution)/shard_map/stack | solution.py:47
  14.6 0.0 copy-start
  14.6 11.7 %all-to-all-start = ((bf16[128,128,512]{2,1,0:T(8,128)(2,1)}), bf16[128,128,512]{2,1,0:T(8,128)(2,1)}, u32[]{:S(2)}, u32[]{:S(2)}) async-start(bf16[128,128,512]{2,1,0:T(8,128)(2,1)} %stack.2), calls=%async_computation | async-start | bytes 33554432 | tf_op jit(solution)/shard_map/all_to_all | solution.py:47
  27.0 242.1 %all-to-all-done = bf16[128,128,512]{2,1,0:T(8,128)(2,1)} async-done(((bf16[128,128,512]{2,1,0:T(8,128)(2,1)}), bf16[128,128,512]{2,1,0:T(8,128)(2,1)}, u32[]{:S(2)}, u32[]{:S(2)}) %all-to-all-start) | async-done | bytes 16777248 | tf_op jit(solution)/shard_map/all_to_all | solution.py:47
  269.2 0.0 copy-done
  269.2 14.6 %fusion.19 = (f32[128]{0:T(128)S(1)}, f32[16384]{0:T(1024)S(1)}, f32[128,16384]{1,0:T(8,128)}) fusion(bf16[128,512]{1,0:T(8,128)(2,1)S(1)} %copy-done, bf16[16384,512]{1,0:T(8,128)(2,1)} %bitcast, f32[]{:T(128)S(6)} %exp.24), kind=kOutput, calls=%fused_computation.34 | convolution fusion | flops 2153758720 | bytes 25362948 | tf_op jit(solution)/shard_map/dot_general | solution.py:54
  283.8 4.7 %exponential_reduce_fusion.1 = (f32[128]{0:T(128)S(1)}, f32[16384]{0:T(1024)S(1)}) fusion(f32[128,16384]{1,0:T(8,128)} %get-tuple-element.22, f32[128]{0:T(128)S(1)} %get-tuple-element.6, f32[16384]{0:T(1024)S(1)} %get-tuple-element.7), kind=kLoop, calls=%fused_computation.9 | loop fusion | flops 8372096 | bytes 8520704 | tf_op jit(solution)/shard_map/reduce_sum | solution.py:58
  288.5 0.7 all_to_all.12
  289.3 15.6 %all-to-all-start.1 = ((f32[128,1,256]{2,1,0:T(1,128)}), f32[128,1,256]{2,1,0:T(1,128)S(1)}, u32[]{:S(2)}, u32[]{:S(2)}) async-start(f32[128,1,256]{2,1,0:T(1,128)} %all_to_all.12), calls=%async_computation.1 | async-start | bytes 262144 | tf_op jit(solution)/shard_map/all_to_all | solution.py:18
  304.9 0.9 constant_dynamic-slice_fusion
  305.8 1.2 gather_fusion
  307.0 0.6 reduce_sum.68
  308.3 0.6 fusion.21
  308.9 5.2 %all-to-all-done.1 = f32[128,1,256]{2,1,0:T(1,128)S(1)} async-done(((f32[128,1,256]{2,1,0:T(1,128)}), f32[128,1,256]{2,1,0:T(1,128)S(1)}, u32[]{:S(2)}, u32[]{:S(2)}) %all-to-all-start.1) | async-done | bytes 131104 | tf_op jit(solution)/shard_map/all_to_all | solution.py:18
  314.2 0.6 fusion.20
  316.1 47.8 %all_gather.6 = f32[16384,2]{0,1:T(2,128)S(1)} all-gather(f32[128,2]{0,1:T(2,128)S(1)} %pad_maximum_fusion.1), channel_id=1, replica_groups=mesh['dp_0'=4,'dp_1'=4,'dp_2'=2,'group'=4] {'dp_0','dp_1','dp_2','group'}, dimensions={0}, use_global_device_ids=true | all-gather | bytes 132096 | tf_op jit(solution)/shard_map/all_gather | solution.py:28
  363.9 0.1 fusion.22
  364.0 6.5 %multiply_reduce_fusion = f32[]{:T(128)} fusion(f32[128,16384]{1,0:T(8,128)} %get-tuple-element.22, s32[128]{0:T(128)S(1)} %iota_add_fusion, f32[16384]{0:T(1024)S(1)} %bitcast.21, f32[128]{0:T(128)S(1)} %get-tuple-element.19), kind=kLoop, calls=%fused_computation.3 | loop fusion | flops 18874368 | bytes 8455172 | tf_op jit(solution)/shard_map/reduce_sum | solution.py:79
  370.5 10.4 %all-reduce.2 = (f32[]{:T(128)}, f32[]{:T(128)}) all-reduce(f32[]{:T(128)S(6)} %sub.87, f32[]{:T(128)} %multiply_reduce_fusion), channel_id=1, replica_groups=mesh['dp_0'=4,'dp_1'=4,'dp_2'=2,'group'=4] {'dp_0'}, use_global_device_ids=true, to_apply=%region_9.10 | all-reduce | flops 2 | bytes 16 | tf_op jit(solution)/shard_map/psum | solution.py:38
  380.9 8.8 %all-reduce.1 = (f32[]{:T(128)}, f32[]{:T(128)}) all-reduce(f32[]{:T(128)} %get-tuple-element.12, f32[]{:T(128)} %get-tuple-element.13), channel_id=1, replica_groups=mesh['dp_0'=4,'dp_1'=4,'dp_2'=2,'group'=4] {'dp_1'}, use_global_device_ids=true, to_apply=%region_10.11 | all-reduce | flops 2 | bytes 16 | tf_op jit(solution)/shard_map/psum | solution.py:38
  389.7 3.1 all-reduce.3
  392.8 10.1 %all-reduce = (f32[]{:T(128)}, f32[]{:T(128)}) all-reduce(f32[]{:T(128)} %get-tuple-element.14, f32[]{:T(128)} %get-tuple-element.15), channel_id=1, replica_groups=mesh['dp_0'=4,'dp_1'=4,'dp_2'=2,'group'=4] {'group'}, use_global_device_ids=true, to_apply=%region_12.13 | all-reduce | flops 2 | bytes 16 | tf_op jit(solution)/shard_map/psum | solution.py:38
  404.2 0.0 copy-start.1
  404.2 12.4 %fusion.12 = bf16[128,512]{1,0:T(8,128)(2,1)} fusion(bf16[16384,512]{1,0:T(8,128)(2,1)} %bitcast, f32[128,16384]{1,0:T(8,128)} %get-tuple-element.22, s32[128]{0:T(128)S(1)} %iota_add_fusion, f32[16384]{0:T(1024)S(1)} %bitcast.22, f32[128]{0:T(128)S(1)} %get-tuple-element.19, f32[]{:T(128)S(6)} %exp.24), kind=kOutput, calls=%fused_computation.19 | convolution fusion | flops 2164391936 | bytes 25363460 | tf_op jit(solution)/shard_map/dot_general | solution.py:82
  416.6 0.0 all-gather.2.cloned.1.call-done
  416.6 0.0 copy-done.1
  416.6 18.5 %fusion.15 = bf16[128,512]{1,0:T(8,128)(2,1)} fusion(bf16[16384,512]{1,0:T(8,128)(2,1)} %all-gather.2.cloned.1.call-done, bf16[128,512]{1,0:T(8,128)(2,1)S(1)} %copy-done.1, s32[128]{0:T(128)S(1)} %iota_add_fusion, f32[128]{0:T(128)S(1)} %get-tuple-element.17, f32[16384]{0:T(1024)S(1)} %bitcast.24, f32[]{:T(128)S(6)} %exp.24), kind=kOutput, calls=%fused_computation.20 | convolution fusion | flops 4313972736 | bytes 17105924 | tf_op jit(solution)/shard_map/dot_general | solution.py:91
  (7 shorter events, 0.1 us)
Async XLA Ops:
  7.2 409.4 %all-gather.2.cloned.1.call-start = ((), (), s32[]{:S(2)}) async-start(), calls=%async_computation.2 | async-start | bytes 16908288 | tf_op jit(solution)/shard_map/all_gather | solution.py:49
  14.6 254.6 %copy-start = (bf16[128,512]{1,0:T(8,128)(2,1)S(1)}, bf16[128,512]{1,0:T(8,128)(2,1)}, u32[]{:S(2)}) copy-start(bf16[128,512]{1,0:T(8,128)(2,1)} %param.3) | copy-start | bytes 393220
  14.6 254.6 %all-to-all-start = ((bf16[128,128,512]{2,1,0:T(8,128)(2,1)}), bf16[128,128,512]{2,1,0:T(8,128)(2,1)}, u32[]{:S(2)}, u32[]{:S(2)}) async-start(bf16[128,128,512]{2,1,0:T(8,128)(2,1)} %stack.2), calls=%async_computation | async-start | bytes 33554432 | tf_op jit(solution)/shard_map/all_to_all | solution.py:47
  289.3 24.9 %all-to-all-start.1 = ((f32[128,1,256]{2,1,0:T(1,128)}), f32[128,1,256]{2,1,0:T(1,128)S(1)}, u32[]{:S(2)}, u32[]{:S(2)}) async-start(f32[128,1,256]{2,1,0:T(1,128)} %all_to_all.12), calls=%async_computation.1 | async-start | bytes 262144 | tf_op jit(solution)/shard_map/all_to_all | solution.py:18
  404.2 12.4 %copy-start.1 = (bf16[128,512]{1,0:T(8,128)(2,1)S(1)}, bf16[128,512]{1,0:T(8,128)(2,1)}, u32[]{:S(2)}) copy-start(bf16[128,512]{1,0:T(8,128)(2,1)} %param.4) | copy-start | bytes 393220
Sparse Core Ops, SparseCore 0:
  11.1 257.7 all-gather.1
